TPU v7x, 32 devices: a whole 2x2x4 slice. The times are simulated.
32 devices in a mesh: rows: 8 (over y, x, core), feat: 4 (over z).
Axes of the slice: x: 2, y: 2, z: 4, core: 2. Of those that a mesh axis runs over, the one named last changes fastest.
Arguments:
- features: bfloat16 [8192, 2048], P('rows', 'feat'), may hold values from -6 to 6
- grad_out: bfloat16 [8192, 2048], P('rows', 'feat'), may hold values from -6 to 6
- eigvecs: float32 [2048, 2048], P('feat', 'rows'), may hold values from -1 to 1, as said below
- eigvals: float32 [2048], replicated, may hold values from 0.1 to 1, as said below
- whiten: bfloat16 [2048, 2048], P(None, 'feat'), may hold values from -0.125 to 0.125
Outputs:
- grad_in: bfloat16 [8192, 2048], P('rows', 'feat')
Inputs may be any that keep to these rules, and one draw needn't show every extreme that they name: `eigvecs`: the columns are orthonormal. `eigvals`: any two entries differ by at least 0.45 / 2048.
All inputs are finite; a program needn't handle non-finite values.
Results may differ from a plain program's by a relative error of at most 0.0074.
Values may be sent and summed in bfloat16 or wider, within the bound.
A program may use at most 128 MiB of HBM per device.

v0:
```python
import jax
import jax.numpy as jnp
from jax import lax
from jax.sharding import PartitionSpec as P


def divided(lam_row, lam_col, first_col):
    on_diag = (
        jnp.arange(lam_row.shape[0], dtype=jnp.int32)[:, None]
        == (first_col + jnp.arange(lam_col.shape[0], dtype=jnp.int32))[None, :]
    )
    root_row = lam_row ** (-0.5)
    root_col = lam_col ** (-0.5)
    gaps_lam = lam_row[:, None] - lam_col[None, :]
    safe_gap = jnp.where(on_diag, jnp.ones_like(gaps_lam), gaps_lam)
    off_diag = (root_row[:, None] - root_col[None, :]) / safe_gap
    diag_vals = -0.5 * lam_row[:, None] ** (-1.5) + jnp.zeros_like(gaps_lam)
    return jnp.where(on_diag, diag_vals, off_diag)


def local(features, grad_out, eigvecs, eigvals, whiten):
    highest = lax.Precision.HIGHEST
    tok_rows, own_cols = features.shape
    row_count = tok_rows * lax.axis_size("rows")
    contract_rows = (((0,), (0,)), ((), ()))
    contract_last = (((1,), (1,)), ((), ()))
    piece_x = lax.all_gather(features, "feat", axis=1, tiled=True)
    piece_g = lax.all_gather(grad_out, "feat", axis=1, tiled=True)
    left_part = lax.dot_general(
        features, piece_g, contract_rows, preferred_element_type=jnp.float32
    )
    right_part = lax.dot_general(
        grad_out, piece_x, contract_rows, preferred_element_type=jnp.float32
    )
    cross_one = left_part
    cross_two = right_part
    sum_x = jnp.sum(piece_x, axis=0, dtype=jnp.float32)
    sum_g = jnp.sum(piece_g, axis=0, dtype=jnp.float32)
    cross_one, cross_two, sum_x, sum_g = (cross_one, cross_two, sum_x, sum_g)
    cross_one, cross_two, sum_x, sum_g = lax.psum((cross_one, cross_two, sum_x, sum_g), "rows")
    both_cross = cross_one + cross_two
    col_mean = sum_x / row_count
    grad_mean = sum_g / row_count
    offset = lax.axis_index("feat") * own_cols
    mean_part = lax.dynamic_slice_in_dim(col_mean, offset, own_cols)
    grad_part = lax.dynamic_slice_in_dim(grad_mean, offset, own_cols)
    sym_gram = 0.5 * (
        both_cross
        - row_count
        * (mean_part[:, None] * grad_mean[None, :] + grad_part[:, None] * col_mean[None, :])
    )
    basis_cols = lax.all_gather(eigvecs, "feat", axis=0, tiled=True)
    basis_block = lax.all_gather(eigvecs, "rows", axis=1, tiled=True)
    narrow = basis_cols.shape[1]
    inner_prod = jnp.dot(sym_gram, basis_cols, precision=highest)
    partial_value = lax.dot_general(basis_block, inner_prod, contract_rows, precision=highest)
    rotated = lax.psum(partial_value, "feat")
    first_col = lax.axis_index("rows") * narrow
    lam_col = lax.dynamic_slice_in_dim(eigvals, first_col, narrow)
    scaled = divided(eigvals, lam_col, first_col) * rotated
    back_rot = jnp.dot(basis_block, scaled, precision=highest)
    sens_own = lax.psum_scatter(
        lax.dot_general(back_rot, basis_cols, contract_last, precision=highest),
        "rows",
        scatter_dimension=0,
        tiled=True,
    )
    scaled_own = (2.0 / row_count * sens_own).astype(jnp.bfloat16)
    sens_scaled = lax.all_gather(scaled_own, "rows", axis=0, tiled=True)
    piece_x = lax.all_gather(features, "feat", axis=1, tiled=True)
    piece_g = lax.all_gather(grad_out, "feat", axis=1, tiled=True)
    shifted = (piece_g.astype(jnp.float32) - grad_mean).astype(jnp.bfloat16)
    centered = (piece_x.astype(jnp.float32) - col_mean).astype(jnp.bfloat16)
    running = jnp.dot(shifted, whiten, preferred_element_type=jnp.float32)
    grad_in = running + lax.dot_general(
        centered, sens_scaled, contract_last, preferred_element_type=jnp.float32
    )
    return grad_in.astype(jnp.bfloat16)


def solution(mesh):
    in_specs = (P("rows", "feat"), P("rows", "feat"), P("feat", "rows"), P(), P(None, "feat"))
    out_specs = P("rows", "feat")
    return jax.shard_map(local, mesh=mesh, in_specs=in_specs, out_specs=out_specs, check_vma=False)
```

profile of v0, /device:TPU:0, one launch (start us, length us, event | category | flops | bytes accessed | tf_op | source)
XLA Modules:
  0.0 552.3 jit_solution(13871746332786428748)
XLA Ops:
  6.5 0.0 copy-start
  6.5 0.0 all-gather.6.cloned.1.call-start
  6.5 0.7 all-gather.6.cloned.1.call-update
  7.3 0.0 all-gather.8.cloned.1.call-start
  7.3 0.7 all-gather.8.cloned.1.call-update
  8.0 0.0 all-gather.10.cloned.1.call-start
  8.1 0.7 all-gather.10.cloned.1.call-update
  8.7 0.0 copy-start.3
  8.8 0.0 all-reduce.6.cloned.1.call-start
  8.8 83.6 %all-gather.6.cloned.1.call-done = bf16[1024,2048]{1,0:T(8,128)(2,1)} async-done(((bf16[1024,512]{1,0:T(8,128)(2,1)}), bf16[1024,2048]{1,0:T(8,128)(2,1)}) %all-gather.6.cloned.1.call-update) | async-done | bytes 4194320 | tf_op jit(solution)/shard_map/all_gather | solution.py:71
  92.4 6.8 %fusion.40 = f32[512,2048]{1,0:T(8,128)} fusion(bf16[1024,512]{1,0:T(8,128)(2,1)} %param.5, bf16[1024,2048]{1,0:T(8,128)(2,1)} %all-gather.6.cloned.1.call-done), kind=kOutput, calls=%fused_computation.51 | convolution fusion | flops 2147483648 | bytes 9437184 | tf_op jit(solution)/shard_map/dot_general | solution.py:29
  99.2 74.0 %all-gather.8.cloned.1.call-done = bf16[1024,2048]{1,0:T(8,128)(2,1)} async-done(((bf16[1024,512]{1,0:T(8,128)(2,1)}), bf16[1024,2048]{1,0:T(8,128)(2,1)}) %all-gather.8.cloned.1.call-update) | async-done | bytes 4194320 | tf_op jit(solution)/shard_map/all_gather | solution.py:70
  173.2 0.0 copy-done.3
  173.2 7.8 %convolution_add_fusion = f32[512,2048]{1,0:T(8,128)} fusion(f32[512,2048]{1,0:T(8,128)} %fusion.40, bf16[1024,512]{1,0:T(8,128)(2,1)S(1)} %copy-done.3, bf16[1024,2048]{1,0:T(8,128)(2,1)} %all-gather.8.cloned.1.call-done), kind=kOutput, calls=%fused_computation.17 | convolution fusion | flops 2148532224 | bytes 13631488 | tf_op jit(solution)/shard_map/dot_general | solution.py:32
  181.0 0.0 all-reduce.6.cloned.1.call-update
  181.1 0.0 all-gather.12.cloned.1.call-start
  181.1 0.5 all-gather.12.cloned.1.call-update
  181.7 0.0 all-reduce.4.cloned.1.call-start
  181.7 0.0 copy-start.1
  181.7 3.0 convert_reduce_fusion
  184.7 0.5 copy-done.1
  185.2 0.6 convert_reduce_fusion.1
  185.8 25.6 %all-reduce = (f32[2048]{0:T(1024)S(1)}, f32[2048]{0:T(1024)S(1)}) all-reduce(f32[2048]{0:T(1024)S(1)} %convert_reduce_fusion, f32[2048]{0:T(1024)S(1)} %convert_reduce_fusion.1), channel_id=1, replica_groups=mesh['rows'=8,'feat'=4] {'rows'}, use_global_device_ids=true, to_apply=%region_3.0 | all-reduce | flops 4096 | bytes 32768 | tf_op jit(solution)/shard_map/psum | solution.py:40
  211.4 0.1 dynamic_slice.10
  211.5 0.1 dynamic_slice.11
  211.6 7.4 %all-gather.10.cloned.1.call-done = f32[2048,256]{1,0:T(8,128)} async-done(((f32[512,256]{1,0:T(8,128)}), f32[2048,256]{1,0:T(8,128)}) %all-gather.10.cloned.1.call-update) | async-done | bytes 2097168 | tf_op jit(solution)/shard_map/all_gather | solution.py:52
  219.0 82.8 %all-reduce.6.cloned.1.call-done = f32[512,2048]{1,0:T(8,128)} async-done(((f32[512,2048]{1,0:T(8,128)}), f32[512,2048]{1,0:T(8,128)}) %all-reduce.6.cloned.1.call-update) | async-done | bytes 4194320 | tf_op jit(solution)/shard_map/psum | solution.py:40
  301.7 6.9 %fusion.6 = f32[512,256]{1,0:T(8,128)S(1)} fusion(f32[2048,256]{1,0:T(8,128)} %all-gather.10.cloned.1.call-done, f32[512,2048]{1,0:T(8,128)} %all-reduce.6.cloned.1.call-done, f32[2048]{0:T(1024)S(1)} %get-tuple-element.11, f32[512]{0:T(512)S(1)} %dynamic_slice.11, f32[2048]{0:T(1024)S(1)} %get-tuple-element.12, f32[512]{0:T(512)S(1)} %dynamic_slice.10), kind=kOutput, calls=%fused_computation.8 | convolution fusion | flops 3227516928 | bytes 6836224 | tf_op jit(solution)/shard_map/dot_general | solution.py:55
  308.6 0.0 copy-start.5
  308.6 32.3 %all-gather.12.cloned.1.call-done = f32[512,2048]{1,0:T(8,128)} async-done(((f32[512,256]{1,0:T(8,128)}), f32[512,2048]{1,0:T(8,128)}) %all-gather.12.cloned.1.call-update) | async-done | bytes 4194320 | tf_op jit(solution)/shard_map/all_gather | solution.py:53
  340.9 10.2 %convolution_bitcast_fusion = f32[2048,256]{1,0:T(8,128)} fusion(f32[512,256]{1,0:T(8,128)S(1)} %fusion.6, f32[512,2048]{1,0:T(8,128)} %all-gather.12.cloned.1.call-done), kind=kOutput, calls=%fused_computation.18 | convolution fusion | flops 3221225472 | bytes 6815744 | tf_op jit(solution)/shard_map/dot_general | solution.py:56
  351.1 0.0 all-reduce.4.cloned.1.call-update
  351.1 0.3 reduce-scatter.2.cloned.1.call-start
  351.4 0.0 copy-done.5
  351.4 0.1 broadcast_power_fusion.1
  351.5 85.9 %all-reduce.4.cloned.1.call-done = f32[2048,256]{1,0:T(8,128)} async-done(((f32[2048,256]{1,0:T(8,128)}), f32[2048,256]{1,0:T(8,128)}) %all-reduce.4.cloned.1.call-update) | async-done | bytes 2097168 | tf_op jit(solution)/shard_map/psum | solution.py:57
  437.4 10.8 %fusion.15 = f32[256,512]{1,0:T(8,128)S(1)} fusion(f32[512,2048]{1,0:T(8,128)} %all-gather.12.cloned.1.call-done, f32[2048,256]{1,0:T(8,128)} %all-reduce.4.cloned.1.call-done, f32[256]{0:T(256)S(1)} %get-tuple-element.8, f32[2048]{0:T(1024)S(1)} %copy-done.5, f32[256]{0:T(256)S(1)} %get-tuple-element.7, f32[2048]{0:T(1024)S(1)} %get-tuple-element.10, ...), kind=kOutput, calls=%fused_computation.20 | convolution fusion | flops 3224895488 | bytes 6843392 | tf_op jit(solution)/shard_map/dot_general | solution.py:61
  448.2 0.0 copy-done.4
  448.2 8.4 %fusion.41 = f32[512,2048]{1,0:T(8,128)} fusion(f32[256,512]{1,0:T(8,128)S(1)} %fusion.15, f32[2048,256]{1,0:T(8,128)S(1)} %copy-done.4), kind=kOutput, calls=%fused_computation.52 | convolution fusion | flops 3221225472 | bytes 6815744 | tf_op jit(solution)/shard_map/dot_general | solution.py:63
  456.6 0.0 reduce-scatter.2.cloned.1.call-update
  456.7 0.3 all-gather.14.cloned.1.call-start
  457.0 50.0 %reduce-scatter.2.cloned.1.call-done = f32[64,2048]{1,0:T(8,128)} async-done(((f32[512,2048]{1,0:T(8,128)}), f32[64,2048]{1,0:T(8,128)}) %reduce-scatter.2.cloned.1.call-update) | async-done | bytes 524304 | tf_op jit(solution)/shard_map/reduce_scatter | solution.py:62
  507.0 1.8 multiply_convert_fusion
  508.8 0.0 all-gather.14.cloned.1.call-update
  508.8 27.9 %all-gather.14.cloned.1.call-done = bf16[512,2048]{1,0:T(8,128)(2,1)} async-done(((bf16[64,2048]{1,0:T(8,128)(2,1)}), bf16[512,2048]{1,0:T(8,128)(2,1)}) %all-gather.14.cloned.1.call-update) | async-done | bytes 2097168 | tf_op jit(solution)/shard_map/all_gather | solution.py:69
  536.7 5.4 fusion.2
  542.1 0.0 copy-done
  542.1 3.3 add_convert_fusion
  (6 shorter events, 0.0 us)
Async XLA Ops:
  6.5 535.6 %copy-start = (bf16[2048,512]{1,0:T(8,128)(2,1)S(1)}, bf16[2048,512]{1,0:T(8,128)(2,1)}, u32[]{:S(2)}) copy-start(bf16[2048,512]{1,0:T(8,128)(2,1)} %param.9) | copy-start | bytes 6291460
  6.5 85.9 %all-gather.6.cloned.1.call-start = ((), (), s32[]{:S(2)}) async-start(), calls=%async_computation.1 | async-start | bytes 5242880 | tf_op jit(solution)/shard_map/all_gather | solution.py:71
  7.3 166.0 %all-gather.8.cloned.1.call-start = ((), (), s32[]{:S(2)}) async-start(), calls=%async_computation.2 | async-start | bytes 5242880 | tf_op jit(solution)/shard_map/all_gather | solution.py:70
  8.0 211.0 %all-gather.10.cloned.1.call-start = ((), (), s32[]{:S(2)}) async-start(), calls=%async_computation.3 | async-start | bytes 2621440 | tf_op jit(solution)/shard_map/all_gather | solution.py:52
  8.7 164.5 %copy-start.3 = (bf16[1024,512]{1,0:T(8,128)(2,1)S(1)}, bf16[1024,512]{1,0:T(8,128)(2,1)}, u32[]{:S(2)}) copy-start(bf16[1024,512]{1,0:T(8,128)(2,1)} %param.6) | copy-start | bytes 3145732
  8.8 293.0 %all-reduce.6.cloned.1.call-start = ((), (), s32[]{:S(2)}) async-start(), calls=%async_computation.8 | async-start | bytes 8388608 | tf_op jit(solution)/shard_map/psum | solution.py:40
  181.1 159.9 %all-gather.12.cloned.1.call-start = ((), (), s32[]{:S(2)}) async-start(), calls=%async_computation.4 | async-start | bytes 4718592 | tf_op jit(solution)/shard_map/all_gather | solution.py:53
  181.7 255.8 %all-reduce.4.cloned.1.call-start = ((), (), s32[]{:S(2)}) async-start(), calls=%async_computation.5 | async-start | bytes 4194304 | tf_op jit(solution)/shard_map/psum | solution.py:57
  181.7 3.5 copy-start.1
  308.6 42.8 %copy-start.5 = (f32[2048]{0:T(1024)S(1)}, f32[2048]{0:T(1024)}, u32[]{:S(2)}) copy-start(f32[2048]{0:T(1024)} %param.8) | copy-start | bytes 24580
  351.1 155.9 %reduce-scatter.2.cloned.1.call-start = ((), (), s32[]{:S(2)}) async-start(), calls=%async_computation.6 | async-start | bytes 4718592 | tf_op jit(solution)/shard_map/reduce_scatter | solution.py:62
  437.4 10.8 %copy-start.4 = (f32[2048,256]{1,0:T(8,128)S(1)}, f32[2048,256]{1,0:T(8,128)}, u32[]{:S(2)}) copy-start(f32[2048,256]{1,0:T(8,128)} %all-gather.10.cloned.1.call-done) | copy-start | bytes 6291460
  456.7 80.1 %all-gather.14.cloned.1.call-start = ((), (), s32[]{:S(2)}) async-start(), calls=%async_computation.7 | async-start | bytes 2359296 | tf_op jit(solution)/shard_map/all_gather | solution.py:69
  536.7 5.4 copy-start.2
Sparse Core Ops, SparseCore 0:
  8.9 83.4 all-gather.5
  94.0 79.2 all-gather.7
  174.8 44.1 all-gather.9
  222.1 79.5 all-reduce.5
  303.5 37.3 all-gather.11
  351.3 86.1 all-reduce.3
  456.8 50.1 reduce-scatter.1
  508.9 27.7 all-gather.13
where the time goes:
time: 552 us
  waiting for transfers between devices  447 us (81%)
  matrix products  59.6 us (11%)
  blocking collectives  25.6 us (5%)
  between operations  13.6 us (2%)
    psum x1, waiting for transfers between devices, local(): rotated = lax.psum(partial_value, 'feat')  85.9 us
    all_gather x1, waiting for transfers between devices, local(): piece_g = lax.all_gather(grad_out, 'feat', axis=1, tiled=True)  83.6 us
    psum x1, waiting for transfers between devices, local(): lax.psum((cross_one, cross_two, sum_x, sum_g), 'rows')  82.8 us
    all_gather x1, waiting for transfers between devices, local(): piece_x = lax.all_gather(features, 'feat', axis=1, tiled=True)  74 us
    reduce_scatter x1, waiting for transfers between devices, local(): lax.psum_scatter(lax.dot_general(back_rot, basis_cols, contract_last, pre...  50 us
    all_gather x1, waiting for transfers between devices, local(): basis_block = lax.all_gather(eigvecs, 'rows', axis=1, tiled=True)  32.3 us
    all_gather x1, waiting for transfers between devices, local(): sens_scaled = lax.all_gather(scaled_own, 'rows', axis=0, tiled=True)  27.9 us
    psum x1, blocking collectives, local(): lax.psum((cross_one, cross_two, sum_x, sum_g), 'rows')  25.6 us
  transfers between devices with their start and end apart: 8, of which 8 were waited for; matrix products, arithmetic and copies ran while one was open for 5% of the time, Pallas kernels for 0%

commit v1 on v0

--- a/solution.py
+++ b/solution.py
@@ -68,7 +68,15 @@
     scaled_own = (2.0 / row_count * sens_own).astype(jnp.bfloat16)
     sens_scaled = lax.all_gather(scaled_own, "rows", axis=0, tiled=True)
     piece_x = lax.all_gather(features, "feat", axis=1, tiled=True)
-    piece_g = lax.all_gather(grad_out, "feat", axis=1, tiled=True)
+    world_n = jax.lax.psum(1, "feat")
+    x_new = grad_out
+    blocks_here = [x_new]
+    kept_arr = [(c - 1, c) for c in range(1, world_n)] + [(world_n - 1, 0)]
+    for _ in range(world_n - 1):
+        x_new = jax.lax.ppermute(x_new, "feat", kept_arr)
+        blocks_here += [x_new]
+    current_value = jnp.concatenate([*reversed(blocks_here)], axis=1)
+    piece_g = jnp.roll(current_value, (jax.lax.axis_index("feat") + 1) * x_new.shape[1], axis=1)
     shifted = (piece_g.astype(jnp.float32) - grad_mean).astype(jnp.bfloat16)
     centered = (piece_x.astype(jnp.float32) - col_mean).astype(jnp.bfloat16)
     running = jnp.dot(shifted, whiten, preferred_element_type=jnp.float32)

time: 552 us -> 596 us (1.080)
  waiting for transfers between devices: 447 us -> 469 us
  local copies, waits for them, and re-layouts: 0.75 us -> 17 us
    ppermute x0 -> x3, waiting for transfers between devices: none -> 51.3 us  [local(): x_new = jax.lax.ppermute(x_new, 'feat', kept_arr)]
    all_gather x1, waiting for transfers between devices: 27.9 us -> 0.01 us  [local(): sens_scaled = lax.all_gather(scaled_own, 'rows', axis=0, tiled=True)]
    unnamed x12 -> x17, local copies, waits for them, and re-layouts: 0.51 us -> 15.7 us
  transfers between devices with their start and end apart: 8 -> 11, of which waited for: 8 -> 9; matrix products, arithmetic and copies ran while one was open for 5% -> 7% of each run, Pallas kernels for 0% -> 0%
where the time goes in v1:
time: 596 us
  waiting for transfers between devices  469 us (79%)
  matrix products  62.7 us (11%)
  blocking collectives  25.6 us (4%)
  local copies, waits for them, and re-layouts  17 us (3%)
  between operations  13.6 us (2%)
    psum x1, waiting for transfers between devices, local(): rotated = lax.psum(partial_value, 'feat')  85.9 us
    all_gather x1, waiting for transfers between devices, local(): piece_g = lax.all_gather(grad_out, 'feat', axis=1, tiled=True)  83.6 us
    psum x1, waiting for transfers between devices, local(): lax.psum((cross_one, cross_two, sum_x, sum_g), 'rows')  82.8 us
    all_gather x1, waiting for transfers between devices, local(): piece_x = lax.all_gather(features, 'feat', axis=1, tiled=True)  74 us
    ppermute x3, waiting for transfers between devices, local(): x_new = jax.lax.ppermute(x_new, 'feat', kept_arr)  51.3 us
    reduce_scatter x1, waiting for transfers between devices, local(): lax.psum_scatter(lax.dot_general(back_rot, basis_cols, contract_last, pre...  49.8 us
    all_gather x1, waiting for transfers between devices, local(): basis_block = lax.all_gather(eigvecs, 'rows', axis=1, tiled=True)  31.4 us
    psum x1, blocking collectives, local(): lax.psum((cross_one, cross_two, sum_x, sum_g), 'rows')  25.6 us
  transfers between devices with their start and end apart: 11, of which 9 were waited for; matrix products, arithmetic and copies ran while one was open for 7% of the time, Pallas kernels for 0%

profile of v1, /device:TPU:0, one launch (start us, length us, event | category | flops | bytes accessed | tf_op | source)
XLA Modules:
  0.0 595.7 jit_solution(17819731853876072754)
XLA Ops:
  6.5 0.7 all-gather.6.cloned.1.call-update
  7.3 0.0 all-gather.8.cloned.1.call-start
  7.3 0.7 all-gather.8.cloned.1.call-update
  8.0 0.0 all-gather.10.cloned.1.call-start
  8.1 0.7 all-gather.10.cloned.1.call-update
  8.8 0.0 all-reduce.6.cloned.1.call-start
  8.8 83.6 %all-gather.6.cloned.1.call-done = bf16[1024,2048]{1,0:T(8,128)(2,1)} async-done(((bf16[1024,512]{1,0:T(8,128)(2,1)}), bf16[1024,2048]{1,0:T(8,128)(2,1)}) %all-gather.6.cloned.1.call-update) | async-done | bytes 4194320 | tf_op jit(solution)/shard_map/all_gather | solution.py:28
  92.4 6.8 %fusion.38 = f32[512,2048]{1,0:T(8,128)} fusion(bf16[1024,512]{1,0:T(8,128)(2,1)} %param.5, bf16[1024,2048]{1,0:T(8,128)(2,1)} %all-gather.6.cloned.1.call-done), kind=kOutput, calls=%fused_computation.60 | convolution fusion | flops 2147483648 | bytes 9437184 | tf_op jit(solution)/shard_map/dot_general | solution.py:29
  99.2 74.0 %all-gather.8.cloned.1.call-done = bf16[1024,2048]{1,0:T(8,128)(2,1)} async-done(((bf16[1024,512]{1,0:T(8,128)(2,1)}), bf16[1024,2048]{1,0:T(8,128)(2,1)}) %all-gather.8.cloned.1.call-update) | async-done | bytes 4194320 | tf_op jit(solution)/shard_map/all_gather | solution.py:70
  173.2 7.8 %convolution_add_fusion = f32[512,2048]{1,0:T(8,128)} fusion(f32[512,2048]{1,0:T(8,128)} %fusion.38, bf16[1024,512]{1,0:T(8,128)(2,1)S(1)} %copy-done.2, bf16[1024,2048]{1,0:T(8,128)(2,1)} %all-gather.8.cloned.1.call-done), kind=kOutput, calls=%fused_computation.17 | convolution fusion | flops 2148532224 | bytes 13631488 | tf_op jit(solution)/shard_map/dot_general | solution.py:32
  181.0 0.0 all-reduce.6.cloned.1.call-update
  181.1 0.0 all-gather.12.cloned.1.call-start
  181.1 0.5 all-gather.12.cloned.1.call-update
  181.6 0.0 all-reduce.4.cloned.1.call-start
  181.7 3.0 convert_reduce_fusion.1
  184.7 0.5 copy-done.1
  185.2 0.6 convert_reduce_fusion
  185.8 25.6 %all-reduce = (f32[2048]{0:T(1024)S(1)}, f32[2048]{0:T(1024)S(1)}) all-reduce(f32[2048]{0:T(1024)S(1)} %convert_reduce_fusion, f32[2048]{0:T(1024)S(1)} %convert_reduce_fusion.1), channel_id=1, replica_groups=mesh['rows'=8,'feat'=4] {'rows'}, use_global_device_ids=true, to_apply=%region_3.0 | all-reduce | flops 4096 | bytes 32768 | tf_op jit(solution)/shard_map/psum | solution.py:40
  211.4 0.1 dynamic_slice.15
  211.5 0.1 dynamic_slice.16
  211.6 7.4 %all-gather.10.cloned.1.call-done = f32[2048,256]{1,0:T(8,128)} async-done(((f32[512,256]{1,0:T(8,128)}), f32[2048,256]{1,0:T(8,128)}) %all-gather.10.cloned.1.call-update) | async-done | bytes 2097168 | tf_op jit(solution)/shard_map/all_gather | solution.py:52
  219.0 82.8 %all-reduce.6.cloned.1.call-done = f32[512,2048]{1,0:T(8,128)} async-done(((f32[512,2048]{1,0:T(8,128)}), f32[512,2048]{1,0:T(8,128)}) %all-reduce.6.cloned.1.call-update) | async-done | bytes 4194320 | tf_op jit(solution)/shard_map/psum | solution.py:40
  301.7 7.8 %fusion.4 = f32[512,256]{1,0:T(8,128)} fusion(f32[2048,256]{1,0:T(8,128)} %all-gather.10.cloned.1.call-done, f32[512,2048]{1,0:T(8,128)} %all-reduce.6.cloned.1.call-done, f32[2048]{0:T(1024)S(1)} %get-tuple-element.11, f32[512]{0:T(512)S(1)} %dynamic_slice.16, f32[2048]{0:T(1024)S(1)} %get-tuple-element.12, f32[512]{0:T(512)S(1)} %dynamic_slice.15), kind=kOutput, calls=%fused_computation.7 | convolution fusion | flops 3227516928 | bytes 6836224 | tf_op jit(solution)/shard_map/dot_general | solution.py:55
  309.6 31.4 %all-gather.12.cloned.1.call-done = f32[512,2048]{1,0:T(8,128)} async-done(((f32[512,256]{1,0:T(8,128)}), f32[512,2048]{1,0:T(8,128)}) %all-gather.12.cloned.1.call-update) | async-done | bytes 4194320 | tf_op jit(solution)/shard_map/all_gather | solution.py:53
  340.9 10.4 %convolution_bitcast_fusion = f32[2048,256]{1,0:T(8,128)} fusion(f32[512,256]{1,0:T(8,128)} %fusion.4, f32[512,2048]{1,0:T(8,128)} %all-gather.12.cloned.1.call-done), kind=kOutput, calls=%fused_computation.18 | convolution fusion | flops 3221225472 | bytes 6815744 | tf_op jit(solution)/shard_map/dot_general | solution.py:56
  351.3 0.0 all-reduce.4.cloned.1.call-update
  351.3 0.3 reduce-scatter.2.cloned.1.call-start
  351.6 0.1 broadcast_power_fusion.1
  351.7 85.9 %all-reduce.4.cloned.1.call-done = f32[2048,256]{1,0:T(8,128)} async-done(((f32[2048,256]{1,0:T(8,128)}), f32[2048,256]{1,0:T(8,128)}) %all-reduce.4.cloned.1.call-update) | async-done | bytes 2097168 | tf_op jit(solution)/shard_map/psum | solution.py:57
  437.6 10.8 %fusion.14 = f32[256,512]{1,0:T(8,128)S(1)} fusion(f32[512,2048]{1,0:T(8,128)} %all-gather.12.cloned.1.call-done, f32[2048,256]{1,0:T(8,128)} %all-reduce.4.cloned.1.call-done, f32[256]{0:T(256)S(1)} %get-tuple-element.8, f32[2048]{0:T(1024)S(1)} %copy-done.4, f32[256]{0:T(256)S(1)} %get-tuple-element.7, f32[2048]{0:T(1024)S(1)} %get-tuple-element.10, ...), kind=kOutput, calls=%fused_computation.20 | convolution fusion | flops 3224895488 | bytes 6843392 | tf_op jit(solution)/shard_map/dot_general | solution.py:61
  448.4 8.4 %fusion.39 = f32[512,2048]{1,0:T(8,128)} fusion(f32[256,512]{1,0:T(8,128)S(1)} %fusion.14, f32[2048,256]{1,0:T(8,128)S(1)} %copy-done.3), kind=kOutput, calls=%fused_computation.61 | convolution fusion | flops 3221225472 | bytes 6815744 | tf_op jit(solution)/shard_map/dot_general | solution.py:63
  456.8 0.0 all-gather.14.cloned.1.call-start
  456.9 0.5 collective-permute-start
  457.3 49.8 %reduce-scatter.2.cloned.1.call-done = f32[64,2048]{1,0:T(8,128)} async-done(((f32[512,2048]{1,0:T(8,128)}), f32[64,2048]{1,0:T(8,128)}) %reduce-scatter.2.cloned.1.call-update) | async-done | bytes 524304 | tf_op jit(solution)/shard_map/reduce_scatter | solution.py:62
  507.2 1.8 multiply_convert_fusion
  509.0 1.5 collective-permute-start.1
  510.5 25.4 %collective-permute-done.1 = bf16[1024,512]{1,0:T(8,128)(2,1)} collective-permute-done((bf16[1024,512]{1,0:T(8,128)(2,1)}, bf16[1024,512]{1,0:T(8,128)(2,1)}, u32[]{:S(2)}, u32[]{:S(2)}) %collective-permute-start.1) | collective-permute-done | bytes 1048608 | tf_op jit(solution)/shard_map/ppermute | solution.py:76
  535.9 26.0 %collective-permute-done.2 = bf16[1024,512]{1,0:T(8,128)(2,1)} collective-permute-done((bf16[1024,512]{1,0:T(8,128)(2,1)}, bf16[1024,512]{1,0:T(8,128)(2,1)}, u32[]{:S(2)}, u32[]{:S(2)}) %collective-permute-start.2) | collective-permute-done | bytes 1048608 | tf_op jit(solution)/shard_map/ppermute | solution.py:76
  561.9 2.3 constant_dynamic-update-slice_fusion.7
  564.2 2.3 constant_dynamic-update-slice_fusion.6
  566.5 2.4 constant_dynamic-update-slice_fusion.5
  568.9 1.1 constant_dynamic-update-slice_fusion.4
  570.0 2.3 constant_dynamic-update-slice_fusion.3
  572.4 2.4 constant_dynamic-update-slice_fusion.2
  574.7 2.4 constant_dynamic-update-slice_fusion.1
  577.1 1.1 constant_dynamic-update-slice_fusion
  578.2 5.2 fusion.2
  583.4 5.5 add_convert_fusion
  (18 shorter events, 0.1 us)
Async XLA Ops:
  6.5 576.9 %copy-start = (bf16[2048,512]{1,0:T(8,128)(2,1)S(1)}, bf16[2048,512]{1,0:T(8,128)(2,1)}, u32[]{:S(2)}) copy-start(bf16[2048,512]{1,0:T(8,128)(2,1)} %param.9) | copy-start | bytes 6291460
  6.5 85.9 %all-gather.6.cloned.1.call-start = ((), (), s32[]{:S(2)}) async-start(), calls=%async_computation.1 | async-start | bytes 5242880 | tf_op jit(solution)/shard_map/all_gather | solution.py:28
  7.3 166.0 %all-gather.8.cloned.1.call-start = ((), (), s32[]{:S(2)}) async-start(), calls=%async_computation.2 | async-start | bytes 5242880 | tf_op jit(solution)/shard_map/all_gather | solution.py:70
  8.0 211.0 %all-gather.10.cloned.1.call-start = ((), (), s32[]{:S(2)}) async-start(), calls=%async_computation.3 | async-start | bytes 2621440 | tf_op jit(solution)/shard_map/all_gather | solution.py:52
  8.7 164.5 %copy-start.2 = (bf16[1024,512]{1,0:T(8,128)(2,1)S(1)}, bf16[1024,512]{1,0:T(8,128)(2,1)}, u32[]{:S(2)}) copy-start(bf16[1024,512]{1,0:T(8,128)(2,1)} %param.6) | copy-start | bytes 3145732
  8.8 293.0 %all-reduce.6.cloned.1.call-start = ((), (), s32[]{:S(2)}) async-start(), calls=%async_computation.8 | async-start | bytes 8388608 | tf_op jit(solution)/shard_map/psum | solution.py:40
  181.1 159.9 %all-gather.12.cloned.1.call-start = ((), (), s32[]{:S(2)}) async-start(), calls=%async_computation.4 | async-start | bytes 4718592 | tf_op jit(solution)/shard_map/all_gather | solution.py:53
  181.6 256.0 %all-reduce.4.cloned.1.call-start = ((), (), s32[]{:S(2)}) async-start(), calls=%async_computation.5 | async-start | bytes 4194304 | tf_op jit(solution)/shard_map/psum | solution.py:57
  181.7 3.5 copy-start.1
  309.6 42.0 %copy-start.4 = (f32[2048]{0:T(1024)S(1)}, f32[2048]{0:T(1024)}, u32[]{:S(2)}) copy-start(f32[2048]{0:T(1024)} %param.8) | copy-start | bytes 24580
  351.3 155.9 %reduce-scatter.2.cloned.1.call-start = ((), (), s32[]{:S(2)}) async-start(), calls=%async_computation.6 | async-start | bytes 4718592 | tf_op jit(solution)/shard_map/reduce_scatter | solution.py:62
  437.6 10.8 %copy-start.3 = (f32[2048,256]{1,0:T(8,128)S(1)}, f32[2048,256]{1,0:T(8,128)}, u32[]{:S(2)}) copy-start(f32[2048,256]{1,0:T(8,128)} %all-gather.10.cloned.1.call-done) | copy-start | bytes 6291460
  456.8 121.3 %all-gather.14.cloned.1.call-start = ((), (), s32[]{:S(2)}) async-start(), calls=%async_computation.7 | async-start | bytes 2359296 | tf_op jit(solution)/shard_map/all_gather | solution.py:69
  456.9 52.1 %collective-permute-start = (bf16[1024,512]{1,0:T(8,128)(2,1)S(1)}, bf16[1024,512]{1,0:T(8,128)(2,1)}, u32[]{:S(2)}, u32[]{:S(2)}) collective-permute-start(bf16[1024,512]{1,0:T(8,128)(2,1)S(1)} %copy-done.2), channel_id=1, source_target_pairs={{0,1},{1,2},{2,3},{3,0},{4,5},{5,6},{6,7},{7,4},{8,9},{9,10},{10,1... | collective-permute-start | bytes 3145736 | tf_op jit(solution)/shard_map/ppermute | solution.py:76
  509.0 26.9 %collective-permute-start.1 = (bf16[1024,512]{1,0:T(8,128)(2,1)}, bf16[1024,512]{1,0:T(8,128)(2,1)}, u32[]{:S(2)}, u32[]{:S(2)}) collective-permute-start(bf16[1024,512]{1,0:T(8,128)(2,1)} %collective-permute-done), channel_id=1, source_target_pairs={{0,1},{1,2},{2,3},{3,0},{4,5},{5,6},{6,7},{7,4},{8,9},{9,10},{10,1... | collective-permute-start | bytes 3145736 | tf_op jit(solution)/shard_map/ppermute | solution.py:76
  535.9 26.0 %collective-permute-start.2 = (bf16[1024,512]{1,0:T(8,128)(2,1)}, bf16[1024,512]{1,0:T(8,128)(2,1)}, u32[]{:S(2)}, u32[]{:S(2)}) collective-permute-start(bf16[1024,512]{1,0:T(8,128)(2,1)} %collective-permute-done.1), channel_id=1, source_target_pairs={{0,1},{1,2},{2,3},{3,0},{4,5},{5,6},{6,7},{7,4},{8,9},{9,10},{10,1... | collective-permute-start | bytes 3145736 | tf_op jit(solution)/shard_map/ppermute | solution.py:76
Sparse Core Ops, SparseCore 0:
  8.9 83.4 all-gather.5
  94.0 79.2 all-gather.7
  174.8 44.1 all-gather.9
  222.1 79.5 all-reduce.5
  303.5 37.3 all-gather.11
  351.4 86.1 all-reduce.3
  456.9 50.1 reduce-scatter.1
  509.1 27.7 all-gather.13
